TPU v7x, 32 devices: a whole 2x2x4 slice. The times are simulated.
32 devices in a mesh: rep: 8 (over y, x, core), tp: 4 (over z).
Axes of the slice: x: 2, y: 2, z: 4, core: 2. Of those that a mesh axis runs over, the one named last changes fastest.
Arguments:
- flat_buffer: bfloat16 [578912256], P(('rep', 'tp')), may hold values from -60 to 60
- shard_pad: int32 [2, 6], replicated, may hold values from 0 to 2
Outputs:
- q_served: bfloat16 [2, 6144, 6144], P(None, 'rep', 'tp')
- q_scale: float32 [2, 48, 6144], P(None, 'rep', 'tp')
- k_served: bfloat16 [2, 6144, 1024], P(None, 'rep', 'tp')
- k_scale: float32 [2, 48, 1024], P(None, 'rep', 'tp')
- v_served: bfloat16 [2, 6144, 1024], P(None, 'rep', 'tp')
- v_scale: float32 [2, 48, 1024], P(None, 'rep', 'tp')
- o_served: bfloat16 [2, 6144, 6144], P(None, 'tp', 'rep')
- o_scale: float32 [2, 48, 6144], P(None, 'tp', 'rep')
- gate_served: bfloat16 [2, 6144, 16384], P(None, 'rep', 'tp')
- gate_scale: float32 [2, 48, 16384], P(None, 'rep', 'tp')
- up_served: bfloat16 [2, 6144, 16384], P(None, 'rep', 'tp')
- up_scale: float32 [2, 48, 16384], P(None, 'rep', 'tp')
All inputs are finite; a program needn't handle non-finite values. Where the computation divides by a largest or mean magnitude, that divisor is 1e-20 or more.
Results may differ from a plain program's by a relative error of at most 0.001.
Values may be sent and summed in bfloat16 or wider, within the bound.
A program may use at most 192 MiB of HBM per device.

v0:
```python
import jax
import jax.numpy as jnp
from jax import lax
from jax.sharding import PartitionSpec as P

D = 6144
KV = 1024
FF = 16384
GROUP = 128
LAYERS = 2


def quantize(served):
    values = served.astype(jnp.float32)
    grouped = values.reshape(values.shape[0] // GROUP, GROUP, values.shape[1])
    peak = jnp.max(jnp.abs(grouped), axis=1) + 1e-06
    scaled = (grouped / peak[:, None, :]).astype(jnp.bfloat16)
    return (scaled.reshape(served.shape), peak)


def column_block(received):
    return received.reshape(-1, received.shape[3]).T


def output_block(received):
    return received.reshape(-1, received.shape[2]).T


def on_device(flat_buffer, shard_pad):
    devices = lax.axis_size("rep") * lax.axis_size("tp")
    widths = (D, KV, KV, D, FF, FF)
    columns = (0, 1, 2, 4, 5)
    tiled = flat_buffer.reshape(flat_buffer.shape[0] // 128, 128)
    offset = jnp.zeros((), jnp.int32)
    pieces = []
    for layer in range(LAYERS):
        layer_pieces = []
        for index in range(6):
            rows = widths[index] // devices
            lines = rows * D // 128
            taken = lax.dynamic_slice_in_dim(tiled, offset, lines, 0)
            layer_pieces.append(taken.reshape(rows, D))
            offset = offset + lines + shard_pad[layer, index]
        pieces.append(layer_pieces)
    blocks = [[None] * 6 for layer in range(LAYERS)]
    for layer in range(LAYERS):
        for index in columns:
            piece = pieces[layer][index]
            received = lax.all_to_all(
                lax.all_to_all(
                    piece.reshape(1, 1, piece.shape[0], D),
                    "rep",
                    split_axis=3,
                    concat_axis=0,
                    tiled=True,
                ),
                "tp",
                split_axis=0,
                concat_axis=1,
                tiled=True,
            )
            blocks[layer][index] = column_block(received)
        piece = pieces[layer][3]
        received_rows = lax.all_to_all(
            piece.reshape(1, piece.shape[0], D), "tp", split_axis=2, concat_axis=0, tiled=True
        )
        blocks[layer][3] = output_block(received_rows)
    results = []
    for index in range(6):
        scaled_list = []
        peak_list = []
        for layer in range(LAYERS):
            scaled, peak = quantize(blocks[layer][index])
            scaled_list.append(scaled)
            peak_list.append(peak)
        results.append(jnp.stack(scaled_list))
        results.append(jnp.stack(peak_list))
    return (
        results[0],
        results[1],
        results[2],
        results[3],
        results[4],
        results[5],
        results[6],
        results[7],
        results[8],
        results[9],
        results[10],
        results[11],
    )


def solution(mesh):
    return jax.shard_map(
        on_device,
        mesh=mesh,
        in_specs=(P(("rep", "tp")), P()),
        out_specs=(
            P(None, "rep", "tp"),
            P(None, "rep", "tp"),
            P(None, "rep", "tp"),
            P(None, "rep", "tp"),
            P(None, "rep", "tp"),
            P(None, "rep", "tp"),
            P(None, "tp", "rep"),
            P(None, "tp", "rep"),
            P(None, "rep", "tp"),
            P(None, "rep", "tp"),
            P(None, "rep", "tp"),
            P(None, "rep", "tp"),
        ),
        check_vma=False,
    )
```

profile of v0, /device:TPU:10, one launch (start us, length us, event | category | flops | bytes accessed | tf_op | source)
XLA Modules:
  0.0 1923.8 jit_solution(5891359268631695627)
XLA Ops:
  16.2 34.4 %reduce.2 = bf16[6144,32]{1,0:T(8,128)(2,1)} reduce(bf16[6144,1,1,32]{3,2,1,0:T(2,128)(2,1)S(1)} %bitcast.370, bf16[]{:T(256)} %broadcast.224), dimensions={1,2}, to_apply=%bitcast.303.reduce_sub_computation | reduce | bytes 786434
  66.9 34.4 %reduce.3 = bf16[6144,32]{1,0:T(8,128)(2,1)} reduce(bf16[6144,1,1,32]{3,2,1,0:T(2,128)(2,1)S(1)} %bitcast.371, bf16[]{:T(256)} %broadcast.224), dimensions={1,2}, to_apply=%bitcast.301.reduce_sub_computation | reduce | bytes 786434
  117.6 34.4 %reduce.4 = bf16[6144,32]{1,0:T(8,128)(2,1)} reduce(bf16[6144,1,1,32]{3,2,1,0:T(2,128)(2,1)S(1)} %bitcast.372, bf16[]{:T(256)} %broadcast.224), dimensions={1,2}, to_apply=%bitcast.307.reduce_sub_computation | reduce | bytes 786434
  165.6 34.4 %reduce.5 = bf16[6144,32]{1,0:T(8,128)(2,1)} reduce(bf16[6144,1,1,32]{3,2,1,0:T(2,128)(2,1)S(1)} %bitcast.373, bf16[]{:T(256)} %broadcast.224), dimensions={1,2}, to_apply=%bitcast.305.reduce_sub_computation | reduce | bytes 786434
  292.3 34.6 %reduce.1 = bf16[6144,192]{1,0:T(8,128)(2,1)S(1)} reduce(bf16[6144,1,1,192]{3,2,1,0:T(2,128)(2,1)} %bitcast.338, bf16[]{:T(256)} %broadcast.224), dimensions={1,2}, to_apply=%bitcast.297.reduce_sub_computation | reduce | bytes 4718594
  354.9 34.6 %reduce = bf16[6144,192]{1,0:T(8,128)(2,1)S(1)} reduce(bf16[6144,1,1,192]{3,2,1,0:T(2,128)(2,1)} %bitcast.339, bf16[]{:T(256)} %broadcast.224), dimensions={1,2}, to_apply=%bitcast.299.reduce_sub_computation | reduce | bytes 4718594
  415.7 34.6 %reduce.6 = bf16[6144,192]{1,0:T(8,128)(2,1)S(1)} reduce(bf16[6144,1,192]{2,1,0:T(2,128)(2,1)} %bitcast.340, bf16[]{:T(256)} %broadcast.224), dimensions={1}, to_apply=%bitcast.293.reduce_sub_computation | reduce | bytes 4718594
  476.1 34.6 %reduce.7 = bf16[6144,192]{1,0:T(8,128)(2,1)S(1)} reduce(bf16[6144,1,192]{2,1,0:T(2,128)(2,1)} %bitcast.341, bf16[]{:T(256)} %broadcast.224), dimensions={1}, to_apply=%bitcast.295.reduce_sub_computation | reduce | bytes 4718594
  522.0 19.1 constant_dynamic-slice_fusion.1
  551.2 26.5 %copy.394 = bf16[1,1,512,6144]{2,1,0,3:T(2,128)(2,1)} copy(bf16[1,1,512,6144]{3,2,1,0:T(8,128)(2,1)} %reshape_reshape.46) | data formatting | bytes 12582912 | tf_op jit(solution)/shard_map/reshape;reshape | solution.py:51
  577.7 41.6 %reduce.10 = bf16[6144,512]{1,0:T(8,128)(2,1)} reduce(bf16[6144,1,1,512]{3,2,1,0:T(2,128)(2,1)} %bitcast.330, bf16[]{:T(256)} %broadcast.224), dimensions={1,2}, to_apply=%bitcast.315.reduce_sub_computation | reduce | bytes 12582914
  645.0 26.5 %copy.400 = bf16[1,1,512,6144]{2,1,0,3:T(2,128)(2,1)} copy(bf16[1,1,512,6144]{3,2,1,0:T(8,128)(2,1)} %reshape_reshape.47) | data formatting | bytes 12582912 | tf_op jit(solution)/shard_map/reshape;reshape | solution.py:51
  671.5 41.7 %reduce.11 = bf16[6144,512]{1,0:T(8,128)(2,1)} reduce(bf16[6144,1,1,512]{3,2,1,0:T(2,128)(2,1)} %bitcast.331, bf16[]{:T(256)} %broadcast.224), dimensions={1,2}, to_apply=%bitcast.313.reduce_sub_computation | reduce | bytes 12582914
  737.7 26.5 %copy.382 = bf16[1,1,512,6144]{2,1,0,3:T(2,128)(2,1)} copy(bf16[1,1,512,6144]{3,2,1,0:T(8,128)(2,1)} %reshape_reshape.44) | data formatting | bytes 12582912 | tf_op jit(solution)/shard_map/reshape;reshape | solution.py:51
  764.2 41.7 %reduce.8 = bf16[6144,512]{1,0:T(8,128)(2,1)} reduce(bf16[6144,1,1,512]{3,2,1,0:T(2,128)(2,1)} %bitcast.332, bf16[]{:T(256)} %broadcast.224), dimensions={1,2}, to_apply=%bitcast.311.reduce_sub_computation | reduce | bytes 12582914
  830.0 26.5 %copy.388 = bf16[1,1,512,6144]{2,1,0,3:T(2,128)(2,1)} copy(bf16[1,1,512,6144]{3,2,1,0:T(8,128)(2,1)} %reshape_reshape.45) | data formatting | bytes 12582912 | tf_op jit(solution)/shard_map/reshape;reshape | solution.py:51
  856.6 41.7 %reduce.9 = bf16[6144,512]{1,0:T(8,128)(2,1)} reduce(bf16[6144,1,1,512]{3,2,1,0:T(2,128)(2,1)} %bitcast.329, bf16[]{:T(256)} %broadcast.224), dimensions={1,2}, to_apply=%bitcast.309.reduce_sub_computation | reduce | bytes 12582914
  920.7 14.0 copy.338
  937.2 45.3 %all-to-all-done.16 = bf16[8,2,196608]{2,1,0:T(2,128)(2,1)} async-done(((bf16[8,2,196608]{2,1,0:T(2,128)(2,1)}), bf16[8,2,196608]{2,1,0:T(2,128)(2,1)}, u32[]{:S(2)}, u32[]{:S(2)}) %all-to-all-start.16) | async-done | bytes 6291488 | tf_op jit(solution)/shard_map/all_to_all | solution.py:50
  1013.6 25.0 %all-to-all-done.3 = bf16[8,1,192,768]{3,2,1,0:T(8,128)(2,1)S(1)} async-done(((bf16[8,1,192,768]{3,2,1,0:T(8,128)(2,1)}), bf16[8,1,192,768]{3,2,1,0:T(8,128)(2,1)S(1)}, u32[]{:S(2)}, u32[]{:S(2)}) %all-to-all-start.3) | async-done | bytes 2359328 | tf_op jit(solution)/shard_map/all_to_all | solution.py:49
  1066.5 30.0 %all-to-all-done.1 = bf16[8,1,192,768]{3,2,1,0:T(8,128)(2,1)} async-done(((bf16[8,1,192,768]{3,2,1,0:T(8,128)(2,1)}), bf16[8,1,192,768]{3,2,1,0:T(8,128)(2,1)}, u32[]{:S(2)}, u32[]{:S(2)}) %all-to-all-start.1) | async-done | bytes 2359328 | tf_op jit(solution)/shard_map/all_to_all | solution.py:49
  1125.2 114.3 %all-to-all-done.19 = bf16[8,1,512,768]{2,3,1,0:T(8,128)(2,1)} async-done(((bf16[8,1,512,768]{2,3,1,0:T(8,128)(2,1)}), bf16[8,1,512,768]{2,3,1,0:T(8,128)(2,1)}, u32[]{:S(2)}, u32[]{:S(2)}) %all-to-all-start.19) | async-done | bytes 6291488 | tf_op jit(solution)/shard_map/all_to_all | solution.py:49
  1711.1 16.6 copy.416
  1905.1 16.6 copy.414
  (286 shorter events, 1083.7 us)
Async XLA Ops:
  54.4 50.7 %all-to-all-start.4 = ((bf16[8,2,12288]{2,1,0:T(2,128)(2,1)}), bf16[8,2,12288]{2,1,0:T(2,128)(2,1)S(1)}, u32[]{:S(2)}, u32[]{:S(2)}) async-start(bf16[8,2,12288]{2,1,0:T(2,128)(2,1)} %reshape.395), calls=%async_computation.4 | async-start | bytes 786432 | tf_op jit(solution)/shard_map/all_to_all | solution.py:50
  105.1 50.7 %copy-start.12 = (bf16[8,2,12288]{2,1,0:T(2,128)(2,1)}, bf16[8,2,12288]{2,1,0:T(2,128)(2,1)S(1)}, u32[]{:S(2)}) copy-start(bf16[8,2,12288]{2,1,0:T(2,128)(2,1)S(1)} %all-to-all-done.4) | copy-start | bytes 1179652
  105.1 50.7 %all-to-all-start.6 = ((bf16[8,2,12288]{2,1,0:T(2,128)(2,1)}), bf16[8,2,12288]{2,1,0:T(2,128)(2,1)}, u32[]{:S(2)}, u32[]{:S(2)}) async-start(bf16[8,2,12288]{2,1,0:T(2,128)(2,1)} %reshape.393), calls=%async_computation.6 | async-start | bytes 786432 | tf_op jit(solution)/shard_map/all_to_all | solution.py:50
  155.8 48.0 %all-to-all-start.8 = ((bf16[8,2,12288]{2,1,0:T(2,128)(2,1)}), bf16[8,2,12288]{2,1,0:T(2,128)(2,1)}, u32[]{:S(2)}, u32[]{:S(2)}) async-start(bf16[8,2,12288]{2,1,0:T(2,128)(2,1)} %reshape.399), calls=%async_computation.8 | async-start | bytes 786432 | tf_op jit(solution)/shard_map/all_to_all | solution.py:50
  203.8 15.1 all-to-all-start.10
  218.9 16.2 all-to-all-start.5
  235.1 16.2 all-to-all-start.7
  251.3 13.4 all-to-all-start.9
  264.7 67.4 %all-to-all-start.11 = ((bf16[8,1,32,768]{3,2,1,0:T(8,128)(2,1)}), bf16[8,1,32,768]{3,2,1,0:T(8,128)(2,1)S(1)}, u32[]{:S(2)}, u32[]{:S(2)}) async-start(bf16[8,1,32,768]{3,2,1,0:T(8,128)(2,1)} %copy.367), calls=%async_computation.11 | async-start | bytes 786432 | tf_op jit(solution)/shard_map/all_to_all | solution.py:49
  332.1 62.6 %all-to-all-start.2 = ((bf16[8,2,73728]{2,1,0:T(2,128)(2,1)}), bf16[8,2,73728]{2,1,0:T(2,128)(2,1)}, u32[]{:S(2)}, u32[]{:S(2)}) async-start(bf16[8,2,73728]{2,1,0:T(2,128)(2,1)} %reshape.389), calls=%async_computation.2 | async-start | bytes 4718592 | tf_op jit(solution)/shard_map/all_to_all | solution.py:50
  394.7 60.0 %all-to-all-start = ((bf16[8,2,73728]{2,1,0:T(2,128)(2,1)}), bf16[8,2,73728]{2,1,0:T(2,128)(2,1)}, u32[]{:S(2)}, u32[]{:S(2)}) async-start(bf16[8,2,73728]{2,1,0:T(2,128)(2,1)} %reshape.391), calls=%async_computation | async-start | bytes 4718592 | tf_op jit(solution)/shard_map/all_to_all | solution.py:50
  454.8 60.4 %all-to-all-start.12 = ((bf16[4,2,147456]{2,1,0:T(2,128)(2,1)}), bf16[4,2,147456]{2,1,0:T(2,128)(2,1)}, u32[]{:S(2)}, u32[]{:S(2)}) async-start(bf16[4,2,147456]{2,1,0:T(2,128)(2,1)} %reshape.385), calls=%async_computation.12 | async-start | bytes 4718592 | tf_op jit(solution)/shard_map/all_to_all | solution.py:64
  515.2 113.6 %all-to-all-start.13 = ((bf16[4,2,147456]{2,1,0:T(2,128)(2,1)}), bf16[4,2,147456]{2,1,0:T(2,128)(2,1)S(1)}, u32[]{:S(2)}, u32[]{:S(2)}) async-start(bf16[4,2,147456]{2,1,0:T(2,128)(2,1)} %reshape.387), calls=%async_computation.13 | async-start | bytes 4718592 | tf_op jit(solution)/shard_map/all_to_all | solution.py:64
  630.3 92.3 %all-to-all-start.18 = ((bf16[8,2,196608]{2,1,0:T(2,128)(2,1)}), bf16[8,2,196608]{2,1,0:T(2,128)(2,1)}, u32[]{:S(2)}, u32[]{:S(2)}) async-start(bf16[8,2,196608]{2,1,0:T(2,128)(2,1)} %reshape.407), calls=%async_computation.18 | async-start | bytes 12582912 | tf_op jit(solution)/shard_map/all_to_all | solution.py:50
  722.6 92.7 %all-to-all-start.20 = ((bf16[8,2,196608]{2,1,0:T(2,128)(2,1)}), bf16[8,2,196608]{2,1,0:T(2,128)(2,1)}, u32[]{:S(2)}, u32[]{:S(2)}) async-start(bf16[8,2,196608]{2,1,0:T(2,128)(2,1)} %reshape.405), calls=%async_computation.20 | async-start | bytes 12582912 | tf_op jit(solution)/shard_map/all_to_all | solution.py:50
  815.3 92.3 %all-to-all-start.14 = ((bf16[8,2,196608]{2,1,0:T(2,128)(2,1)}), bf16[8,2,196608]{2,1,0:T(2,128)(2,1)}, u32[]{:S(2)}, u32[]{:S(2)}) async-start(bf16[8,2,196608]{2,1,0:T(2,128)(2,1)} %reshape.403), calls=%async_computation.14 | async-start | bytes 12582912 | tf_op jit(solution)/shard_map/all_to_all | solution.py:50
  907.6 74.9 %all-to-all-start.16 = ((bf16[8,2,196608]{2,1,0:T(2,128)(2,1)}), bf16[8,2,196608]{2,1,0:T(2,128)(2,1)}, u32[]{:S(2)}, u32[]{:S(2)}) async-start(bf16[8,2,196608]{2,1,0:T(2,128)(2,1)} %reshape.401), calls=%async_computation.16 | async-start | bytes 12582912 | tf_op jit(solution)/shard_map/all_to_all | solution.py:50
  982.6 56.1 %all-to-all-start.3 = ((bf16[8,1,192,768]{3,2,1,0:T(8,128)(2,1)}), bf16[8,1,192,768]{3,2,1,0:T(8,128)(2,1)S(1)}, u32[]{:S(2)}, u32[]{:S(2)}) async-start(bf16[8,1,192,768]{3,2,1,0:T(8,128)(2,1)} %copy.339), calls=%async_computation.3 | async-start | bytes 4718592 | tf_op jit(solution)/shard_map/all_to_all | solution.py:49
  1038.6 57.9 %all-to-all-start.1 = ((bf16[8,1,192,768]{3,2,1,0:T(8,128)(2,1)}), bf16[8,1,192,768]{3,2,1,0:T(8,128)(2,1)}, u32[]{:S(2)}, u32[]{:S(2)}) async-start(bf16[8,1,192,768]{3,2,1,0:T(8,128)(2,1)} %copy.332), calls=%async_computation.1 | async-start | bytes 4718592 | tf_op jit(solution)/shard_map/all_to_all | solution.py:49
  1096.5 142.9 %all-to-all-start.19 = ((bf16[8,1,512,768]{2,3,1,0:T(8,128)(2,1)}), bf16[8,1,512,768]{2,3,1,0:T(8,128)(2,1)}, u32[]{:S(2)}, u32[]{:S(2)}) async-start(bf16[8,1,512,768]{2,3,1,0:T(8,128)(2,1)} %bitcast.345), calls=%async_computation.19 | async-start | bytes 12582912 | tf_op jit(solution)/shard_map/all_to_all | solution.py:49
  1239.4 172.2 %all-to-all-start.21 = ((bf16[8,1,512,768]{2,3,1,0:T(8,128)(2,1)}), bf16[8,1,512,768]{2,3,1,0:T(8,128)(2,1)}, u32[]{:S(2)}, u32[]{:S(2)}) async-start(bf16[8,1,512,768]{2,3,1,0:T(8,128)(2,1)} %bitcast.342), calls=%async_computation.21 | async-start | bytes 12582912 | tf_op jit(solution)/shard_map/all_to_all | solution.py:49
  1411.6 185.0 %all-to-all-start.15 = ((bf16[8,1,512,768]{2,3,1,0:T(8,128)(2,1)}), bf16[8,1,512,768]{2,3,1,0:T(8,128)(2,1)}, u32[]{:S(2)}, u32[]{:S(2)}) async-start(bf16[8,1,512,768]{2,3,1,0:T(8,128)(2,1)} %bitcast.344), calls=%async_computation.15 | async-start | bytes 12582912 | tf_op jit(solution)/shard_map/all_to_all | solution.py:49
  1596.6 187.3 %all-to-all-start.17 = ((bf16[8,1,512,768]{2,3,1,0:T(8,128)(2,1)}), bf16[8,1,512,768]{2,3,1,0:T(8,128)(2,1)}, u32[]{:S(2)}, u32[]{:S(2)}) async-start(bf16[8,1,512,768]{2,3,1,0:T(8,128)(2,1)} %bitcast.343), calls=%async_computation.17 | async-start | bytes 12582912 | tf_op jit(solution)/shard_map/all_to_all | solution.py:49
  1877.1 22.1 %slice-start.2 = ((s8[6291456]{0:T(1024)(128)(4,1)}), s8[2097152]{0:T(1024)(128)(4,1)S(1)}, s32[]{:S(2)}) async-start(s8[6291456]{0:T(1024)(128)(4,1)} %bitcast.354), calls=%async_computation.24 | async-start | bytes 4194304
  (20 other events, 134.7 us)
where the time goes:
time: 1950 us; the launch traced here: 1920 us
  local copies, waits for them, and re-layouts  923 us (47%)
  other arithmetic  653 us (33%)
  waiting for transfers between devices  217 us (11%)
  starting transfers between devices  120 us (6%)
    unnamed x14, other arithmetic  443 us
    unnamed x91, local copies, waits for them, and re-layouts  274 us
    another operation x20, local copies, waits for them, and re-layouts, on_device(): piece.reshape(1, 1, piece.shape[0], D)  204 us
    all_to_all x10, waiting for transfers between devices, on_device(): lax.all_to_all(lax.all_to_all(piece.reshape(1, 1, piece.shape[0], D), 're...  171 us
    div x24, local copies, waits for them, and re-layouts, quantize(): scaled = (grouped / peak[:, None, :]).astype(jnp.bfloat16)  124 us
    abs x12, local copies, waits for them, and re-layouts, quantize(): peak = jnp.max(jnp.abs(grouped), axis=1) + 1e-06  84.2 us
    all_to_all x10, starting transfers between devices, on_device(): lax.all_to_all(lax.all_to_all(piece.reshape(1, 1, piece.shape[0], D), 're...  63.1 us
    convert_element_type x14, local copies, waits for them, and re-layouts, quantize(): values = served.astype(jnp.float32)  61.9 us
  transfers between devices with their start and end apart: 22, of which 5 were waited for; matrix products, arithmetic and copies ran while one was open for 71% of the time, Pallas kernels for 0%

commit v1 on v0

v1 whole, which is shorter than its diff:
```python
import functools

import jax
import jax.numpy as jnp
from jax import lax
from jax.experimental import pallas as pl
from jax.experimental.pallas import tpu as pltpu
from jax.sharding import PartitionSpec as P

D = 6144
KV = 1024
FF = 16384
GROUP = 128
LAYERS = 2


def quantize_kernel(order, *refs):
    received, scaled, scale = refs[0], refs[-2], refs[-1]
    group = pl.program_id(0)
    parts = [received[where + (0,)].astype(jnp.float32) for where in order]
    served = jnp.concatenate(parts, axis=0).T
    peak = jnp.max(jnp.abs(served), axis=0, keepdims=True) + 1e-06
    scaled[0] = (served / peak).astype(jnp.bfloat16)
    scale[0, pl.ds(group, 1), :] = peak


def quantize(received, layer, earlier):
    lead = received.shape[:-3]
    groups, rows, width = received.shape[-3:]
    if len(lead) == 2:
        order = [(inner, outer) for outer in range(lead[1]) for inner in range(lead[0])]
    else:
        order = [(inner,) for inner in range(lead[0])]
    total = len(order) * rows
    block = lead + (1, rows, width)
    zeros = (0,) * len(lead)
    return pl.pallas_call(
        functools.partial(quantize_kernel, order),
        grid=(groups,),
        in_specs=[pl.BlockSpec(block, lambda g: zeros + (g, 0, 0))]
        + [pl.BlockSpec(memory_space=pl.ANY)] * len(earlier),
        out_specs=[
            pl.BlockSpec((1, GROUP, total), lambda g: (layer, g, 0)),
            pl.BlockSpec((1, groups, total), lambda g: (layer, 0, 0)),
        ],
        out_shape=[
            jax.ShapeDtypeStruct((LAYERS, groups * GROUP, total), jnp.bfloat16),
            jax.ShapeDtypeStruct((LAYERS, groups, total), jnp.float32),
        ],
        input_output_aliases={1 + i: i for i in range(len(earlier))},
        cost_estimate=pl.CostEstimate(
            flops=20 * groups * GROUP * total,
            bytes_accessed=4 * groups * GROUP * total,
            transcendentals=0,
        ),
    )(received, *earlier)


def on_device(flat_buffer, shard_pad):
    reps = lax.axis_size("rep")
    tps = lax.axis_size("tp")
    devices = reps * tps
    widths = (D, KV, KV, D, FF, FF)
    tiled = flat_buffer.reshape(flat_buffer.shape[0] // GROUP, GROUP)
    offsets = []
    offset = jnp.zeros((), jnp.int32)
    for layer in range(LAYERS):
        for index in range(6):
            offsets.append(offset)
            offset = offset + widths[index] // devices * D // GROUP + shard_pad[layer, index]
    outputs = [()] * 6
    for layer in range(LAYERS):
        for index in (4, 5, 0, 3, 1, 2):
            rows = widths[index] // devices
            lines = D // GROUP
            taken = lax.dynamic_slice_in_dim(tiled, offsets[layer * 6 + index], rows * lines, 0)
            piece = taken.reshape(rows, lines, GROUP).transpose(1, 0, 2)
            if index == 3:
                received = lax.all_to_all(piece, "tp", split_axis=0, concat_axis=0, tiled=True)
                received = received.reshape(tps, lines // tps, rows, GROUP)
            else:
                received = lax.all_to_all(piece, "rep", split_axis=0, concat_axis=0, tiled=True)
                received = received.reshape(reps, lines // reps, rows, GROUP)
                received = lax.all_to_all(received, "tp", split_axis=0, concat_axis=0, tiled=True)
                received = received.reshape(tps, reps // tps, lines // reps, rows, GROUP)
            outputs[index] = quantize(received, layer, tuple(outputs[index]))
    return tuple(array for pair in outputs for array in pair)


def solution(mesh):
    column = P(None, "rep", "tp")
    row = P(None, "tp", "rep")
    return jax.shard_map(
        on_device,
        mesh=mesh,
        in_specs=(P(("rep", "tp")), P()),
        out_specs=(column,) * 6 + (row,) * 2 + (column,) * 4,
        check_vma=False,
    )
```

time: 1950 us -> 1310 us (0.67)
  local copies, waits for them, and re-layouts: 923 us -> 79.5 us
  blocking collectives: 0 us -> 665 us
  other arithmetic: 653 us -> 0 us
  waiting for transfers between devices: 217 us -> 394 us
  Pallas kernels: 0 us -> 77.7 us
  starting transfers between devices: 120 us -> 73.5 us
    all_to_all x0 -> x9, blocking collectives: none -> 665 us  [the longest x7 577 us: on_device(): lax.all_to_all(received, 'tp', split_axis=0, concat_axis=0, tiled=True)]
    unnamed x14 -> x0, other arithmetic: 443 us -> none
    unnamed x91 -> x18, local copies, waits for them, and re-layouts: 274 us -> 12.2 us
    another operation x24 -> x0, local copies, waits for them, and re-layouts: 236 us -> none  [the longest x20 204 us: on_device(): piece.reshape(1, 1, piece.shape[0], D)]
    all_to_all x22 -> x13, waiting for transfers between devices: 217 us -> 394 us  [the longest x8 255 us: on_device(): lax.all_to_all(piece, 'rep', split_axis=0, concat_axis=0, tiled=True)]
    div x24 -> x0, local copies, waits for them, and re-layouts: 124 us -> none  [quantize(): scaled = (grouped / peak[:, None, :]).astype(jnp.bfloat16)]
    all_to_all x18 -> x0, local copies, waits for them, and re-layouts: 113 us -> none  [the longest x12 51.5 us: on_device(): lax.all_to_all(piece.reshape(1, 1, piece.shape[0], D), 'rep', split_axis=...]
    convert_element_type x22 -> x0, other arithmetic: 99 us -> none  [the longest x12 58.5 us: quantize(): scaled = (grouped / peak[:, None, :]).astype(jnp.bfloat16)]
  transfers between devices with their start and end apart: 22 -> 13, of which waited for: 5 -> 12; matrix products, arithmetic and copies ran while one was open for 71% -> 5% of each run, Pallas kernels for 0% -> 5%
where the time goes in v1:
time: 1310 us; the launch traced here: 1300 us
  blocking collectives  665 us (51%)
  waiting for transfers between devices  394 us (30%)
  local copies, waits for them, and re-layouts  79.5 us (6%)
  Pallas kernels  77.7 us (6%)
  starting transfers between devices  73.5 us (6%)
    all_to_all x7, blocking collectives, on_device(): lax.all_to_all(received, 'tp', split_axis=0, concat_axis=0, tiled=True)  577 us
    all_to_all x8, waiting for transfers between devices, on_device(): lax.all_to_all(piece, 'rep', split_axis=0, concat_axis=0, tiled=True)  255 us
    all_to_all x2, blocking collectives, on_device(): lax.all_to_all(piece, 'rep', split_axis=0, concat_axis=0, tiled=True)  88.3 us
    pallas_call x12, Pallas kernels, quantize(): pl.pallas_call(functools.partial(quantize_kernel, order), grid=(groups,),...  77.7 us
    all_to_all x2, waiting for transfers between devices, on_device(): lax.all_to_all(piece, 'tp', split_axis=0, concat_axis=0, tiled=True)  74.8 us
    all_to_all x3, waiting for transfers between devices, on_device(): lax.all_to_all(received, 'tp', split_axis=0, concat_axis=0, tiled=True)  64.3 us
    all_to_all x8, starting transfers between devices, on_device(): lax.all_to_all(piece, 'rep', split_axis=0, concat_axis=0, tiled=True)  42.3 us
    transpose x12, local copies, waits for them, and re-layouts, on_device(): piece = taken.reshape(rows, lines, GROUP).transpose(1, 0, 2)  39.5 us
  transfers between devices with their start and end apart: 13, of which 12 were waited for; matrix products, arithmetic and copies ran while one was open for 5% of the time, Pallas kernels for 5%

profile of v1, /device:TPU:10, one launch (start us, length us, event | category | flops | bytes accessed | tf_op | source)
XLA Modules:
  0.0 1299.3 jit_solution(7797727800659231753)
XLA Ops:
  46.7 11.4 all_to_all.110
  58.1 15.0 %all_to_all.111 = bf16[8,6,32,128]{3,2,1,0:T(8,128)(2,1)} all-to-all(bf16[8,6,32,128]{3,2,1,0:T(8,128)(2,1)S(1)} %bitcast.93), channel_id=1, replica_groups=mesh['rep'=8,'tp'=4] {'tp'}, dimensions={0} | all-to-all | bytes 786432 | tf_op jit(solution)/shard_map/all_to_all | solution.py:84
  73.1 13.9 %all_to_all.112 = bf16[8,6,32,128]{3,2,1,0:T(8,128)(2,1)} all-to-all(bf16[8,6,32,128]{3,2,1,0:T(8,128)(2,1)S(1)} %bitcast.94), channel_id=1, replica_groups=mesh['rep'=8,'tp'=4] {'tp'}, dimensions={0} | all-to-all | bytes 786432 | tf_op jit(solution)/shard_map/all_to_all | solution.py:84
  122.0 24.2 %all-to-all-done = bf16[48,192,128]{2,1,0:T(8,128)(2,1)S(1)} async-done(((bf16[48,192,128]{2,1,0:T(8,128)(2,1)}), bf16[48,192,128]{2,1,0:T(8,128)(2,1)S(1)}, u32[]{:S(2)}, u32[]{:S(2)}) %all-to-all-start) | async-done | bytes 2359328 | tf_op jit(solution)/shard_map/all_to_all | solution.py:82
  155.7 24.4 %all-to-all-done.2 = bf16[48,192,128]{2,1,0:T(8,128)(2,1)} async-done(((bf16[48,192,128]{2,1,0:T(8,128)(2,1)}), bf16[48,192,128]{2,1,0:T(8,128)(2,1)}, u32[]{:S(2)}, u32[]{:S(2)}) %all-to-all-start.2) | async-done | bytes 2359328 | tf_op jit(solution)/shard_map/all_to_all | solution.py:82
  189.8 47.4 %all-to-all-done.13 = bf16[48,192,128]{2,1,0:T(8,128)(2,1)S(1)} async-done(((bf16[48,192,128]{2,1,0:T(8,128)(2,1)}), bf16[48,192,128]{2,1,0:T(8,128)(2,1)S(1)}, u32[]{:S(2)}, u32[]{:S(2)}) %all-to-all-start.13) | async-done | bytes 2359328 | tf_op jit(solution)/shard_map/all_to_all | solution.py:79
  246.7 17.2 %constant_dynamic-slice_fusion = (bf16[24576,128]{1,0:T(8,128)(2,1)S(1)}, bf16[24576,128]{1,0:T(8,128)(2,1)}, bf16[24576,128]{1,0:T(8,128)(2,1)}, bf16[24576,128]{1,0:T(8,128)(2,1)}) fusion(bf16[141336,128]{1,0:T(8,128)(2,1)} %bitcast.73, s32[]{:T(128)S(6)} %select_n.43, s32[]{:T(128)S(6)} %select_n.42, s32[]{:T(128)S(6)} %select_n.41, s32[]{:T(128)S(6)} %select_n.40), kind=kLoop, calls=%fused_computation | loop fusion | bytes 50331664 | tf_op jit(solution)/shard_map/dynamic_slice | solution.py:76
  268.1 27.5 %all-to-all-done.12 = bf16[48,192,128]{2,1,0:T(8,128)(2,1)S(1)} async-done(((bf16[48,192,128]{2,1,0:T(8,128)(2,1)}), bf16[48,192,128]{2,1,0:T(8,128)(2,1)S(1)}, u32[]{:S(2)}, u32[]{:S(2)}) %all-to-all-start.12) | async-done | bytes 2359328 | tf_op jit(solution)/shard_map/all_to_all | solution.py:79
  309.1 61.4 %all-to-all-done.20 = bf16[48,512,128]{2,1,0:T(8,128)(2,1)} async-done(((bf16[48,512,128]{2,1,0:T(8,128)(2,1)}), bf16[48,512,128]{2,1,0:T(8,128)(2,1)}, u32[]{:S(2)}, u32[]{:S(2)}) %all-to-all-start.20) | async-done | bytes 6291488 | tf_op jit(solution)/shard_map/all_to_all | solution.py:82
  383.7 63.1 %all-to-all-done.18 = bf16[48,512,128]{2,1,0:T(8,128)(2,1)} async-done(((bf16[48,512,128]{2,1,0:T(8,128)(2,1)}), bf16[48,512,128]{2,1,0:T(8,128)(2,1)}, u32[]{:S(2)}, u32[]{:S(2)}) %all-to-all-start.18) | async-done | bytes 6291488 | tf_op jit(solution)/shard_map/all_to_all | solution.py:82
  460.0 63.1 %all-to-all-done.16 = bf16[48,512,128]{2,1,0:T(8,128)(2,1)} async-done(((bf16[48,512,128]{2,1,0:T(8,128)(2,1)}), bf16[48,512,128]{2,1,0:T(8,128)(2,1)}, u32[]{:S(2)}, u32[]{:S(2)}) %all-to-all-start.16) | async-done | bytes 6291488 | tf_op jit(solution)/shard_map/all_to_all | solution.py:82
  523.1 76.9 %all_to_all.113 = bf16[48,512,128]{2,1,0:T(8,128)(2,1)} all-to-all(bf16[48,512,128]{2,1,0:T(8,128)(2,1)} %copy.76), channel_id=1, replica_groups=mesh['rep'=8,'tp'=4] {'rep'}, dimensions={0} | all-to-all | bytes 12582912 | tf_op jit(solution)/shard_map/all_to_all | solution.py:82
  600.0 58.9 %all_to_all.114 = bf16[8,6,192,128]{3,2,1,0:T(8,128)(2,1)} all-to-all(bf16[8,6,192,128]{3,2,1,0:T(8,128)(2,1)S(1)} %bitcast.85), channel_id=1, replica_groups=mesh['rep'=8,'tp'=4] {'tp'}, dimensions={0} | all-to-all | bytes 4718592 | tf_op jit(solution)/shard_map/all_to_all | solution.py:84
  658.9 57.9 %all_to_all.115 = bf16[8,6,192,128]{3,2,1,0:T(8,128)(2,1)} all-to-all(bf16[8,6,192,128]{3,2,1,0:T(8,128)(2,1)} %bitcast.12), channel_id=1, replica_groups=mesh['rep'=8,'tp'=4] {'tp'}, dimensions={0} | all-to-all | bytes 4718592 | tf_op jit(solution)/shard_map/all_to_all | solution.py:84
  716.8 143.8 %all_to_all.116 = bf16[8,6,512,128]{3,2,1,0:T(8,128)(2,1)} all-to-all(bf16[8,6,512,128]{3,2,1,0:T(8,128)(2,1)} %bitcast.57), channel_id=1, replica_groups=mesh['rep'=8,'tp'=4] {'tp'}, dimensions={0} | all-to-all | bytes 12582912 | tf_op jit(solution)/shard_map/all_to_all | solution.py:84
  860.5 143.9 %all_to_all.117 = bf16[8,6,512,128]{3,2,1,0:T(8,128)(2,1)} all-to-all(bf16[8,6,512,128]{3,2,1,0:T(8,128)(2,1)} %bitcast.53), channel_id=1, replica_groups=mesh['rep'=8,'tp'=4] {'tp'}, dimensions={0} | all-to-all | bytes 12582912 | tf_op jit(solution)/shard_map/all_to_all | solution.py:84
  1004.4 143.8 %all_to_all.118 = bf16[8,6,512,128]{3,2,1,0:T(8,128)(2,1)} all-to-all(bf16[8,6,512,128]{3,2,1,0:T(8,128)(2,1)} %bitcast.48), channel_id=1, replica_groups=mesh['rep'=8,'tp'=4] {'tp'}, dimensions={0} | all-to-all | bytes 12582912 | tf_op jit(solution)/shard_map/all_to_all | solution.py:84
  1174.8 8.4 shard_map.127
  1183.2 8.4 shard_map.128
  1205.5 8.3 shard_map.131
  1213.8 8.3 shard_map.132
  1223.9 8.3 shard_map.129
  1232.2 57.0 %all-to-all-done.15 = bf16[8,6,512,128]{3,2,1,0:T(8,128)(2,1)} async-done(((bf16[8,6,512,128]{3,2,1,0:T(8,128)(2,1)}), bf16[8,6,512,128]{3,2,1,0:T(8,128)(2,1)}, u32[]{:S(2)}, u32[]{:S(2)}) %all-to-all-start.15) | async-done | bytes 6291488 | tf_op jit(solution)/shard_map/all_to_all | solution.py:84
  1289.2 8.3 shard_map.130
  (58 shorter events, 189.5 us)
Async XLA Ops:
  11.5 11.1 all-to-all-start.6
  22.6 11.7 all-to-all-start.4
  34.3 12.4 all-to-all-start.10
  87.0 13.1 %all-to-all-start.11 = ((bf16[8,6,32,128]{3,2,1,0:T(8,128)(2,1)}), bf16[8,6,32,128]{3,2,1,0:T(8,128)(2,1)S(1)}, u32[]{:S(2)}, u32[]{:S(2)}) async-start(bf16[8,6,32,128]{3,2,1,0:T(8,128)(2,1)} %bitcast.32), calls=%async_computation.11 | async-start | bytes 786432 | tf_op jit(solution)/shard_map/all_to_all | solution.py:84
  100.1 11.3 copy-start.4
  100.1 13.3 %all-to-all-start.9 = ((bf16[8,6,32,128]{3,2,1,0:T(8,128)(2,1)}), bf16[8,6,32,128]{3,2,1,0:T(8,128)(2,1)S(1)}, u32[]{:S(2)}, u32[]{:S(2)}) async-start(bf16[8,6,32,128]{3,2,1,0:T(8,128)(2,1)} %bitcast.28), calls=%async_computation.9 | async-start | bytes 786432 | tf_op jit(solution)/shard_map/all_to_all | solution.py:84
  113.5 8.5 copy-start.5
  113.5 32.7 %all-to-all-start = ((bf16[48,192,128]{2,1,0:T(8,128)(2,1)}), bf16[48,192,128]{2,1,0:T(8,128)(2,1)S(1)}, u32[]{:S(2)}, u32[]{:S(2)}) async-start(bf16[48,192,128]{2,1,0:T(8,128)(2,1)} %copy.68), calls=%async_computation | async-start | bytes 4718592 | tf_op jit(solution)/shard_map/all_to_all | solution.py:82
  146.2 33.8 %copy-start.2 = (bf16[48,192,128]{2,1,0:T(8,128)(2,1)}, bf16[48,192,128]{2,1,0:T(8,128)(2,1)S(1)}, u32[]{:S(2)}) copy-start(bf16[48,192,128]{2,1,0:T(8,128)(2,1)S(1)} %all-to-all-done) | copy-start | bytes 7077892
  146.2 33.8 %all-to-all-start.2 = ((bf16[48,192,128]{2,1,0:T(8,128)(2,1)}), bf16[48,192,128]{2,1,0:T(8,128)(2,1)}, u32[]{:S(2)}, u32[]{:S(2)}) async-start(bf16[48,192,128]{2,1,0:T(8,128)(2,1)} %copy.69), calls=%async_computation.2 | async-start | bytes 4718592 | tf_op jit(solution)/shard_map/all_to_all | solution.py:82
  180.0 57.1 %all-to-all-start.13 = ((bf16[48,192,128]{2,1,0:T(8,128)(2,1)}), bf16[48,192,128]{2,1,0:T(8,128)(2,1)S(1)}, u32[]{:S(2)}, u32[]{:S(2)}) async-start(bf16[48,192,128]{2,1,0:T(8,128)(2,1)} %copy.75), calls=%async_computation.13 | async-start | bytes 4718592 | tf_op jit(solution)/shard_map/all_to_all | solution.py:79
  237.2 1.4 copy-start.1
  238.5 57.1 %all-to-all-start.12 = ((bf16[48,192,128]{2,1,0:T(8,128)(2,1)}), bf16[48,192,128]{2,1,0:T(8,128)(2,1)S(1)}, u32[]{:S(2)}, u32[]{:S(2)}) async-start(bf16[48,192,128]{2,1,0:T(8,128)(2,1)} %copy.74), calls=%async_computation.12 | async-start | bytes 4718592 | tf_op jit(solution)/shard_map/all_to_all | solution.py:79
  295.6 1.4 copy-start
  297.0 73.5 %all-to-all-start.20 = ((bf16[48,512,128]{2,1,0:T(8,128)(2,1)}), bf16[48,512,128]{2,1,0:T(8,128)(2,1)}, u32[]{:S(2)}, u32[]{:S(2)}) async-start(bf16[48,512,128]{2,1,0:T(8,128)(2,1)} %copy.79), calls=%async_computation.20 | async-start | bytes 12582912 | tf_op jit(solution)/shard_map/all_to_all | solution.py:82
  370.5 76.3 %all-to-all-start.18 = ((bf16[48,512,128]{2,1,0:T(8,128)(2,1)}), bf16[48,512,128]{2,1,0:T(8,128)(2,1)}, u32[]{:S(2)}, u32[]{:S(2)}) async-start(bf16[48,512,128]{2,1,0:T(8,128)(2,1)} %copy.78), calls=%async_computation.18 | async-start | bytes 12582912 | tf_op jit(solution)/shard_map/all_to_all | solution.py:82
  446.8 76.3 %all-to-all-start.16 = ((bf16[48,512,128]{2,1,0:T(8,128)(2,1)}), bf16[48,512,128]{2,1,0:T(8,128)(2,1)}, u32[]{:S(2)}, u32[]{:S(2)}) async-start(bf16[48,512,128]{2,1,0:T(8,128)(2,1)} %copy.77), calls=%async_computation.16 | async-start | bytes 12582912 | tf_op jit(solution)/shard_map/all_to_all | solution.py:82
  460.0 140.0 %copy-start.3 = (bf16[48,192,128]{2,1,0:T(8,128)(2,1)S(1)}, bf16[48,192,128]{2,1,0:T(8,128)(2,1)}, u32[]{:S(2)}) copy-start(bf16[48,192,128]{2,1,0:T(8,128)(2,1)} %copy-done.2) | copy-start | bytes 7077892
  1148.2 140.9 %all-to-all-start.15 = ((bf16[8,6,512,128]{3,2,1,0:T(8,128)(2,1)}), bf16[8,6,512,128]{3,2,1,0:T(8,128)(2,1)}, u32[]{:S(2)}, u32[]{:S(2)}) async-start(bf16[8,6,512,128]{3,2,1,0:T(8,128)(2,1)} %bitcast.74), calls=%async_computation.15 | async-start | bytes 12582912 | tf_op jit(solution)/shard_map/all_to_all | solution.py:84
